TPU v7x, 32 devices: a whole 2x2x4 slice. The times are simulated.
32 devices in a mesh: expert: 4 (over z), tensor: 8 (over y, x, core).
Axes of the slice: x: 2, y: 2, z: 4, core: 2. Of those that a mesh axis runs over, the one named last changes fastest.
Arguments:
- expert_inputs: bfloat16 [8, 64, 4096], P('expert'), may hold values from -6 to 6
- gates: float32 [8, 64], P('expert'), may hold values from 0.2 to 1
- chosen_tokens: int32 [8, 64], replicated, may hold values from 0 to 4095, as said below
- w_gate: bfloat16 [8, 4096, 1792], P('expert', None, 'tensor'), may hold values from -0.09375 to 0.09375
- w_up: bfloat16 [8, 4096, 1792], P('expert', None, 'tensor'), may hold values from -0.09375 to 0.09375
- w_down: bfloat16 [8, 1792, 4096], P('expert', 'tensor'), may hold values from -0.125 to 0.125
- residual: bfloat16 [4096, 4096], P(('expert', 'tensor')), may hold values from -6 to 6
- norm_gain: float32 [4096], replicated, may hold values from 0.5 to 1.5
- w_qkv: bfloat16 [4096, 12288], P(None, 'tensor'), may hold values from -0.09375 to 0.09375
Outputs:
- stream: bfloat16 [4096, 4096], P(('expert', 'tensor'))
- projected: bfloat16 [4096, 12288], P('expert', 'tensor')
Inputs may be any that keep to these rules, and one draw needn't show every extreme that they name: `chosen_tokens`: each row holds 64 different token indices; at most 4 of a row lie in one block of 128 consecutive tokens, and in every draw some block holds 4 tokens of every row.
All inputs are finite; a program needn't handle non-finite values.
Results may differ from a plain program's by a relative error of at most 0.005.
Values may be sent and summed in bfloat16 or wider, within the bound.
A program may use at most 128 MiB of HBM per device.

v0:
```python
import jax
import jax.numpy as jnp
from jax import lax
from jax.sharding import PartitionSpec as P

MOST = 4


def rank_within(target_owner):
    count_rows = target_owner.shape[0]
    same_owner = target_owner[:, None] == target_owner[None, :]
    earlier_rows = jnp.arange(count_rows)[None, :] < jnp.arange(count_rows)[:, None]
    return jnp.sum((same_owner & earlier_rows).astype(jnp.int32), axis=1)


def per_device(
    expert_inputs, gates, chosen_tokens, w_gate, w_up, w_down, residual, norm_gain, w_qkv
):
    expert_count = lax.axis_size("expert")
    tensor_count = lax.axis_size("tensor")
    devices_all = expert_count * tensor_count
    owner_index = lax.axis_index("expert") * tensor_count + lax.axis_index("tensor")
    local_experts = expert_inputs.shape[0]
    slot_count = expert_inputs.shape[1]
    feature_width = expert_inputs.shape[2]
    tok_rows = residual.shape[0]
    slot_depth = local_experts * MOST
    gate_part = jnp.einsum(
        "ecd,edf->ecf", expert_inputs, w_gate, preferred_element_type=jnp.float32
    )
    up_part = jnp.einsum("ecd,edf->ecf", expert_inputs, w_up, preferred_element_type=jnp.float32)
    hidden = (jax.nn.silu(gate_part) * up_part).astype(jnp.bfloat16)
    partial_value = (
        jnp.einsum("ecf,efd->ecd", hidden, w_down, preferred_element_type=jnp.float32)
        * gates[:, :, None]
    )
    expert_rows = partial_value.reshape(-1, feature_width)
    row_total = expert_rows.shape[0]
    my_tokens = lax.dynamic_slice_in_dim(
        chosen_tokens, lax.axis_index("expert") * local_experts, local_experts, 0
    ).reshape(-1)
    target_owner = my_tokens // tok_rows
    place_rank = rank_within(target_owner)
    sorting_key = target_owner % tensor_count * expert_count + target_owner // tensor_count
    target_slot = sorting_key * slot_depth + place_rank
    source = (
        jnp.full((devices_all * slot_depth,), row_total, jnp.int32)
        .at[target_slot]
        .set(jnp.arange(row_total, dtype=jnp.int32))
    )
    padded = jnp.concatenate([expert_rows, jnp.zeros((1, feature_width), jnp.float32)], axis=0)
    buffer = jnp.take(padded, source, axis=0)
    reduced = lax.psum_scatter(buffer, "tensor", scatter_dimension=0, tiled=True)
    arrived = lax.all_to_all(
        reduced.reshape(expert_count, slot_depth, feature_width),
        "expert",
        split_axis=0,
        concat_axis=0,
        tiled=True,
    )
    accumulated_rows = arrived.reshape(expert_count * slot_depth, feature_width)
    group_tokens = chosen_tokens.reshape(expert_count, local_experts * slot_count)
    group_owner = group_tokens // tok_rows
    group_rank = jax.vmap(rank_within)(group_owner)
    is_mine = group_owner == owner_index
    group_key = jnp.where(
        is_mine,
        jnp.arange(expert_count, dtype=jnp.int32)[:, None] * slot_depth + group_rank,
        expert_count * slot_depth,
    )
    slot_offset = (
        jnp.full((expert_count * slot_depth,), -1, jnp.int32)
        .at[group_key.reshape(-1)]
        .set((group_tokens % tok_rows).reshape(-1), mode="drop")
    )
    placement_table = (
        jnp.arange(tok_rows, dtype=jnp.int32)[:, None] == slot_offset[None, :]
    ).astype(jnp.float32)
    combined = residual.astype(jnp.float32) + jnp.dot(
        placement_table,
        accumulated_rows,
        precision=lax.Precision.HIGHEST,
        preferred_element_type=jnp.float32,
    )
    stream = combined.astype(jnp.bfloat16)
    scale_rows = lax.rsqrt(jnp.mean(combined * combined, axis=-1, keepdims=True) + 1e-06)
    normed = (combined * scale_rows * norm_gain[None, :]).astype(jnp.bfloat16)
    projected = jnp.dot(
        lax.all_gather(normed, "tensor", axis=0, tiled=True),
        w_qkv,
        preferred_element_type=jnp.float32,
    ).astype(jnp.bfloat16)
    return (stream, projected)


def solution(mesh):
    return jax.shard_map(
        per_device,
        mesh=mesh,
        in_specs=(
            P("expert", None, None),
            P("expert", None),
            P(),
            P("expert", None, "tensor"),
            P("expert", None, "tensor"),
            P("expert", "tensor", None),
            P(("expert", "tensor"), None),
            P(),
            P(None, "tensor"),
        ),
        out_specs=(P(("expert", "tensor"), None), P("expert", "tensor")),
        check_vma=False,
    )
```

profile of v0, /device:TPU:0, one launch (start us, length us, event | category | flops | bytes accessed | tf_op | source)
XLA Modules:
  0.0 184.1 jit_solution(11455417475515096686)
XLA Ops:
  7.2 0.0 copy-start
  7.2 0.0 copy-start.4
  7.2 0.0 reduce-scatter.2.cloned.1.call-start
  7.2 0.8 constant_dynamic-slice_fusion
  8.0 0.1 reshape.423
  8.1 0.1 reshape.422
  8.2 0.2 convert_reduce_fusion.1
  8.4 1.0 scatter_custom_fusion.1
  9.4 0.0 copy-done
  9.4 3.3 %fusion.20 = f32[2,64,224]{2,1,0:T(8,128)S(1)} fusion(bf16[2,64,4096]{2,1,0:T(8,128)(2,1)S(1)} %copy-done, bf16[2,4096,224]{1,2,0:T(8,128)(2,1)} %param.12), kind=kOutput, calls=%fused_computation.70 | convolution fusion | flops 234881024 | bytes 4833280 | tf_op jit(solution)/shard_map/ecd,edf->ecf/dot_general | solution.py:28
  12.7 0.0 copy-done.4
  12.7 6.5 %convolution_multiply_fusion = f32[2,64,4096]{2,1,0:T(8,128)} fusion(bf16[2,224,4096]{2,1,0:T(8,128)(2,1)} %param.14, bf16[2,64,4096]{2,1,0:T(8,128)(2,1)S(1)} %copy-done, bf16[2,4096,224]{1,2,0:T(8,128)(2,1)} %param.13, f32[2,64]{1,0:T(2,128)S(1)} %copy-done.4, f32[2,64,224]{2,1,0:T(8,128)S(1)} %fusion.20), kind=kOutput, calls=%fused_computation.4 | convolution fusion | flops 470458368 | bytes 10600960 | tf_op jit(solution)/shard_map/ecf,efd->ecd/dot_general | solution.py:34
  19.2 1.8 concatenate.3
  21.1 3.8 %gather_fusion = f32[256,4096]{1,0:T(8,128)} fusion(f32[129,4096]{1,0:T(8,128)S(1)} %concatenate.3, s32[1024]{0:T(1024)S(1)} %pad_clamp_fusion), kind=kCustom, calls=%fused_computation | custom fusion | bytes 8389632 | tf_op jit(solution)/shard_map/jit(_take)/gather | solution.py:52
  24.9 4.7 %broadcast_select_fusion = f32[256,4096]{1,0:T(8,128)} fusion(f32[256,4096]{1,0:T(8,128)} %gather_fusion, pred[256]{0:T(512)(128)(4,1)S(1)} %compare_and_fusion), kind=kLoop, calls=%fused_computation.8 | loop fusion | flops 1048576 | bytes 8388864 | tf_op jit(solution)/shard_map/jit(_take)/select_n | solution.py:52
  29.6 0.0 copy-start.2
  29.6 0.0 copy-start.1
  29.6 0.0 copy-start.3
  29.6 0.0 reduce-scatter.2.cloned.1.call-update
  29.6 0.7 copy-done.2
  30.3 0.1 reshape.420
  30.4 53.3 %reduce-scatter.2.cloned.1.call-done = f32[32,4096]{1,0:T(8,128)} async-done(((f32[256,4096]{1,0:T(8,128)}), f32[32,4096]{1,0:T(8,128)}) %reduce-scatter.2.cloned.1.call-update) | async-done | bytes 524304 | tf_op jit(solution)/shard_map/reduce_scatter | solution.py:53
  83.7 4.6 %all-to-all-start = ((f32[4,8,4096]{2,1,0:T(8,128)}), f32[4,8,4096]{2,1,0:T(8,128)S(1)}, u32[]{:S(2)}, u32[]{:S(2)}) async-start(f32[4,8,4096]{2,1,0:T(8,128)} %bitcast.25), calls=%async_computation.1 | async-start | bytes 1048576 | tf_op jit(solution)/shard_map/all_to_all | solution.py:54
  88.2 0.0 all-gather.2.cloned.1.call-start
  88.2 0.2 convert_reduce_fusion
  88.5 0.1 reshape.419
  88.6 0.1 reshape.421
  88.7 0.1 broadcast_add_fusion
  88.8 2.4 %scatter_custom_fusion = s32[32]{0:T(128)S(1)} fusion(s32[512]{0:T(512)S(1)} %bitcast.27, s32[512]{0:T(512)S(1)} %add_select_fusion, s32[]{:T(128)} %constant.88.clone.1), kind=kCustom, calls=%fused_computation.67 | custom fusion | bytes 132 | tf_op jit(solution)/shard_map/scatter | solution.py:74
  91.2 11.4 %all-to-all-done = f32[4,8,4096]{2,1,0:T(8,128)S(1)} async-done(((f32[4,8,4096]{2,1,0:T(8,128)}), f32[4,8,4096]{2,1,0:T(8,128)S(1)}, u32[]{:S(2)}, u32[]{:S(2)}) %all-to-all-start) | async-done | bytes 524320 | tf_op jit(solution)/shard_map/all_to_all | solution.py:54
  102.6 0.0 copy-done.1
  102.6 1.3 multiply_reduce_fusion
  103.8 0.0 copy-done.3
  103.9 1.7 multiply_convert_fusion
  105.5 0.0 all-gather.2.cloned.1.call-update
  105.6 52.5 %all-gather.2.cloned.1.call-done = bf16[1024,4096]{1,0:T(8,128)(2,1)} async-done(((bf16[128,4096]{1,0:T(8,128)(2,1)}), bf16[1024,4096]{1,0:T(8,128)(2,1)}) %all-gather.2.cloned.1.call-update) | async-done | bytes 8388624 | tf_op jit(solution)/shard_map/all_gather | solution.py:89
  158.1 19.1 %convolution_convert_fusion = bf16[1024,1536]{1,0:T(8,128)(2,1)} fusion(bf16[1024,4096]{1,0:T(8,128)(2,1)} %all-gather.2.cloned.1.call-done, bf16[4096,1536]{1,0:T(8,128)(2,1)} %param.17), kind=kOutput, calls=%fused_computation.5 | convolution fusion | flops 12886474752 | bytes 24117248 | tf_op jit(solution)/shard_map/dot_general | solution.py:88
  (12 shorter events, 0.1 us)
Async XLA Ops:
  7.2 2.3 %copy-start = (bf16[2,64,4096]{2,1,0:T(8,128)(2,1)S(1)}, bf16[2,64,4096]{2,1,0:T(8,128)(2,1)}, u32[]{:S(2)}) copy-start(bf16[2,64,4096]{2,1,0:T(8,128)(2,1)} %param.9) | copy-start | bytes 3145732
  7.2 5.6 %copy-start.4 = (f32[2,64]{1,0:T(2,128)S(1)}, f32[2,64]{1,0:T(2,128)}, u32[]{:S(2)}) copy-start(f32[2,64]{1,0:T(2,128)} %param.10) | copy-start | bytes 1540
  7.2 76.5 %reduce-scatter.2.cloned.1.call-start = ((), (), s32[]{:S(2)}) async-start(), calls=%async_computation.2 | async-start | bytes 4718592 | tf_op jit(solution)/shard_map/reduce_scatter | solution.py:53
  29.6 0.7 copy-start.2
  29.6 73.0 %copy-start.1 = (bf16[128,4096]{1,0:T(8,128)(2,1)S(1)}, bf16[128,4096]{1,0:T(8,128)(2,1)}, u32[]{:S(2)}) copy-start(bf16[128,4096]{1,0:T(8,128)(2,1)} %param.15) | copy-start | bytes 3145732
  29.6 74.3 %copy-start.3 = (f32[4096]{0:T(1024)S(1)}, f32[4096]{0:T(1024)}, u32[]{:S(2)}) copy-start(f32[4096]{0:T(1024)} %param.16) | copy-start | bytes 49156
  83.7 18.9 %all-to-all-start = ((f32[4,8,4096]{2,1,0:T(8,128)}), f32[4,8,4096]{2,1,0:T(8,128)S(1)}, u32[]{:S(2)}, u32[]{:S(2)}) async-start(f32[4,8,4096]{2,1,0:T(8,128)} %bitcast.25), calls=%async_computation.1 | async-start | bytes 1048576 | tf_op jit(solution)/shard_map/all_to_all | solution.py:54
  88.2 69.8 %all-gather.2.cloned.1.call-start = ((), (), s32[]{:S(2)}) async-start(), calls=%async_computation.3 | async-start | bytes 9437184 | tf_op jit(solution)/shard_map/all_gather | solution.py:89
Sparse Core Ops, SparseCore 0:
  29.7 53.8 reduce-scatter.1
  105.7 52.3 all-gather.1
where the time goes:
time: 184 us
  waiting for transfers between devices  117 us (64%)
  matrix products  30.2 us (16%)
  between operations  14.2 us (8%)
  local copies, waits for them, and re-layouts  10.9 us (6%)
  other arithmetic  6.99 us (4%)
  starting transfers between devices  4.62 us (3%)
    reduce_scatter x1, waiting for transfers between devices, per_device(): lax.psum_scatter(buffer, 'tensor', scatter_dimension=0, tiled=True)  53.3 us
    all_gather x1, waiting for transfers between devices, per_device(): lax.all_gather(normed, 'tensor', axis=0, tiled=True)  52.5 us
    dot_general x1, matrix products, per_device(): jnp.dot(lax.all_gather(normed, 'tensor', axis=0, tiled=True), w_qkv, pref...  19.1 us
    all_to_all x1, waiting for transfers between devices, per_device(): lax.all_to_all(reduced.reshape(expert_count, slot_depth, feature_width),...  11.4 us
    dot_general x1, matrix products, per_device(): jnp.einsum('ecf,efd->ecd', hidden, w_down, preferred_element_type=jnp.flo...  6.48 us
    select_n x2, other arithmetic, per_device(): buffer = jnp.take(padded, source, axis=0)  4.7 us
    all_to_all x1, starting transfers between devices, per_device(): lax.all_to_all(reduced.reshape(expert_count, slot_depth, feature_width),...  4.58 us
    gather x1, local copies, waits for them, and re-layouts, per_device(): buffer = jnp.take(padded, source, axis=0)  3.83 us
  transfers between devices with their start and end apart: 3, of which 3 were waited for; matrix products, arithmetic and copies ran while one was open for 2% of the time, Pallas kernels for 0%

commit v1 on v0

v1 whole, which is shorter than its diff:
```python
import functools

import jax
import jax.numpy as jnp
from jax import lax
from jax.experimental import pallas as pl
from jax.experimental.pallas import tpu as pltpu
from jax.sharding import PartitionSpec as P

MOST = 4


def finish_kernel(
    row_steps,
    owner_ref,
    slots_ref,
    residual_ref,
    rows_ref,
    gain_ref,
    weight_ref,
    stream_ref,
    projected_ref,
    combined_ref,
    normed_ref,
):
    step = pl.program_id(0)
    tok_rows, feature_width = residual_ref.shape
    chunk = 512

    @pl.when(step < row_steps)
    def _():
        tokens = lax.broadcasted_iota(jnp.int32, (tok_rows, slots_ref.shape[1]), 0)
        placement = jnp.where(slots_ref[...] == tokens + step * tok_rows, 1.0, 0.0).astype(
            jnp.bfloat16
        )
        squares = jnp.zeros((tok_rows, 128), jnp.float32)
        for start in range(0, feature_width, chunk):
            cols = pl.ds(start, chunk)
            combined = residual_ref[:, cols].astype(jnp.float32) + jnp.dot(
                placement, rows_ref[:, cols], preferred_element_type=jnp.float32
            )
            combined_ref[:, cols] = combined
            for part in range(0, chunk, 128):
                piece = combined[:, part : part + 128]
                squares = squares + piece * piece
        mean = jnp.sum(squares, axis=1, keepdims=True) / feature_width
        scale = lax.rsqrt(mean + 1e-06)
        begin = pl.multiple_of(step * tok_rows, tok_rows)
        for start in range(0, feature_width, chunk):
            cols = pl.ds(start, chunk)
            normed_ref[pl.ds(begin, tok_rows), cols] = (
                combined_ref[:, cols] * scale * gain_ref[:, cols]
            ).astype(jnp.bfloat16)

        @pl.when(step == owner_ref[0])
        def _():
            stream_ref[...] = combined_ref[...].astype(jnp.bfloat16)

    @pl.when(step >= row_steps)
    def _():
        projected_ref[...] = jnp.dot(
            normed_ref[...], weight_ref[...], preferred_element_type=jnp.float32
        ).astype(jnp.bfloat16)


def finish(owner, slots, residual_all, rows, gain, w_qkv, tok_rows):
    total_rows, feature_width = residual_all.shape
    columns = w_qkv.shape[1]
    tile = 256
    row_steps = total_rows // tok_rows
    col_steps = columns // tile
    slot_total = rows.shape[0]
    return pl.pallas_call(
        functools.partial(finish_kernel, row_steps),
        grid=(row_steps + col_steps,),
        in_specs=[
            pl.BlockSpec(memory_space=pltpu.SMEM),
            pl.BlockSpec((1, slot_total), lambda i: (0, 0)),
            pl.BlockSpec((tok_rows, feature_width), lambda i: (jnp.minimum(i, row_steps - 1), 0)),
            pl.BlockSpec((slot_total, feature_width), lambda i: (0, 0)),
            pl.BlockSpec((1, feature_width), lambda i: (0, 0)),
            pl.BlockSpec((feature_width, tile), lambda i: (0, jnp.maximum(i - row_steps, 0))),
        ],
        out_specs=[
            pl.BlockSpec((tok_rows, feature_width), lambda i: (0, 0)),
            pl.BlockSpec((total_rows, tile), lambda i: (0, jnp.maximum(i - row_steps, 0))),
        ],
        out_shape=[
            jax.ShapeDtypeStruct((tok_rows, feature_width), jnp.bfloat16),
            jax.ShapeDtypeStruct((total_rows, columns), jnp.bfloat16),
        ],
        scratch_shapes=[
            pltpu.VMEM((tok_rows, feature_width), jnp.float32),
            pltpu.VMEM((total_rows, feature_width), jnp.bfloat16),
        ],
        compiler_params=pltpu.CompilerParams(
            vmem_limit_bytes=60 * 1024 * 1024, dimension_semantics=("arbitrary",)
        ),
        cost_estimate=pl.CostEstimate(
            flops=2 * total_rows * feature_width * (columns + slot_total),
            bytes_accessed=2 * (feature_width * columns + total_rows * columns),
            transcendentals=0,
        ),
    )(owner, slots, residual_all, rows, gain, w_qkv)


def per_device(
    expert_inputs, gates, chosen_tokens, w_gate, w_up, w_down, residual, norm_gain, w_qkv
):
    expert_count = lax.axis_size("expert")
    tensor_count = lax.axis_size("tensor")
    my_group = lax.axis_index("expert")
    local_experts, slot_count, feature_width = expert_inputs.shape
    tok_rows = residual.shape[0]
    group_rows = tok_rows * tensor_count
    keep = min(slot_count, MOST * tensor_count)

    residual_all = lax.all_gather(residual, "tensor", axis=0, tiled=True)

    dest = chosen_tokens // group_rows
    earlier = jnp.arange(slot_count)[None, :] < jnp.arange(slot_count)[:, None]
    rank = jnp.sum(
        ((dest[:, :, None] == dest[:, None, :]) & earlier[None]).astype(jnp.int32), axis=2
    )
    kept = jnp.arange(keep, dtype=jnp.int32)
    mine = jnp.where(dest == my_group, rank, -1)
    token_at = jnp.sum(
        jnp.where(
            mine[:, None, :] == kept[None, :, None],
            (chosen_tokens % group_rows)[:, None, :] + 1,
            0,
        ),
        axis=2,
    ).reshape(1, -1) - 1

    gate_part = jnp.einsum(
        "ecd,edf->ecf", expert_inputs, w_gate, preferred_element_type=jnp.float32
    )
    up_part = jnp.einsum("ecd,edf->ecf", expert_inputs, w_up, preferred_element_type=jnp.float32)
    hidden = (jax.nn.silu(gate_part) * up_part).astype(jnp.bfloat16)
    partial_value = (
        jnp.einsum("ecf,efd->ecd", hidden, w_down, preferred_element_type=jnp.float32)
        * gates[:, :, None]
    ).astype(jnp.bfloat16)
    row_total = local_experts * slot_count
    arrived = lax.all_to_all(
        partial_value.reshape(row_total, feature_width),
        "tensor",
        split_axis=1,
        concat_axis=0,
        tiled=True,
    ).reshape(tensor_count, local_experts, slot_count, -1)
    summed = jnp.sum(arrived.astype(jnp.float32), axis=0).astype(jnp.bfloat16)

    local_dest = lax.dynamic_slice_in_dim(dest, my_group * local_experts, local_experts, 0)
    local_rank = lax.dynamic_slice_in_dim(rank, my_group * local_experts, local_experts, 0)
    send_table = (
        (local_dest[None, :, None, :] == jnp.arange(expert_count)[:, None, None, None])
        & (local_rank[None, :, None, :] == kept[None, None, :, None])
    ).astype(jnp.bfloat16)
    outgoing = jnp.einsum("zlkj,ljf->zlkf", send_table, summed)
    incoming = lax.all_to_all(
        outgoing.reshape(expert_count, local_experts * keep, -1),
        "expert",
        split_axis=0,
        concat_axis=0,
        tiled=True,
    ).reshape(expert_count * local_experts * keep, -1)
    rows = lax.all_gather(incoming, "tensor", axis=1, tiled=True)

    return finish(
        lax.axis_index("tensor").reshape(1),
        token_at,
        residual_all,
        rows,
        norm_gain[None, :],
        w_qkv,
        tok_rows,
    )


def solution(mesh):
    return jax.shard_map(
        per_device,
        mesh=mesh,
        in_specs=(
            P("expert", None, None),
            P("expert", None),
            P(),
            P("expert", None, "tensor"),
            P("expert", None, "tensor"),
            P("expert", "tensor", None),
            P(("expert", "tensor"), None),
            P(),
            P(None, "tensor"),
        ),
        out_specs=(P(("expert", "tensor"), None), P("expert", "tensor")),
        check_vma=False,
    )
```

time: 184 us -> 168 us (0.913)
  Pallas kernels: 0 us -> 26.1 us
  matrix products: 30.2 us -> 8.65 us
  waiting for transfers between devices: 117 us -> 97.6 us
  blocking collectives: 0 us -> 11.9 us
  local copies, waits for them, and re-layouts: 10.9 us -> 3.55 us
  other arithmetic: 6.99 us -> 0.73 us
    reduce_scatter x1 -> x0, waiting for transfers between devices: 53.3 us -> none  [per_device(): lax.psum_scatter(buffer, 'tensor', scatter_dimension=0, tiled=True)]
    all_gather x1 -> x2, waiting for transfers between devices: 52.5 us -> 82 us  [the longest x1 56.2 us: per_device(): residual_all = lax.all_gather(residual, 'tensor', axis=0, tiled=True)]
    pallas_call x0 -> x1, Pallas kernels: none -> 26.1 us  [finish(): pl.pallas_call(functools.partial(finish_kernel, row_steps), grid=(row_ste...]
    dot_general x2 -> x1, matrix products: 20.4 us -> 0.2 us  [per_device(): outgoing = jnp.einsum('zlkj,ljf->zlkf', send_table, summed)]
    all_to_all x0 -> x1, blocking collectives: none -> 11.9 us  [per_device(): lax.all_to_all(outgoing.reshape(expert_count, local_experts * keep, -1),...]
    select_n x7 -> x2, other arithmetic: 4.78 us -> 0.02 us  [the longest x1 0.01 us: per_device(): mine = jnp.where(dest == my_group, rank, -1)]
    gather x1 -> x0, local copies, waits for them, and re-layouts: 3.83 us -> none  [per_device(): buffer = jnp.take(padded, source, axis=0)]
    all_to_all x1, waiting for transfers between devices: 11.4 us -> 14.9 us  [per_device(): lax.all_to_all(partial_value.reshape(row_total, feature_width), 'tensor',...]
  transfers between devices with their start and end apart: 3 -> 3, of which waited for: 3 -> 3; matrix products, arithmetic and copies ran while one was open for 2% -> 1% of each run, Pallas kernels for 0% -> 0%
where the time goes in v1:
time: 168 us
  waiting for transfers between devices  97.6 us (58%)
  Pallas kernels  26.1 us (16%)
  between operations  14.2 us (8%)
  blocking collectives  11.9 us (7%)
  matrix products  8.65 us (5%)
  starting transfers between devices  5.28 us (3%)
  local copies, waits for them, and re-layouts  3.55 us (2%)
    all_gather x1, waiting for transfers between devices, per_device(): residual_all = lax.all_gather(residual, 'tensor', axis=0, tiled=True)  56.2 us
    pallas_call x1, Pallas kernels, finish(): pl.pallas_call(functools.partial(finish_kernel, row_steps), grid=(row_ste...  26.1 us
    all_gather x1, waiting for transfers between devices, per_device(): rows = lax.all_gather(incoming, 'tensor', axis=1, tiled=True)  25.8 us
    all_to_all x1, waiting for transfers between devices, per_device(): lax.all_to_all(partial_value.reshape(row_total, feature_width), 'tensor',...  14.9 us
    all_to_all x1, blocking collectives, per_device(): lax.all_to_all(outgoing.reshape(expert_count, local_experts * keep, -1),...  11.9 us
    all_to_all x1, starting transfers between devices, per_device(): lax.all_to_all(partial_value.reshape(row_total, feature_width), 'tensor',...  5.2 us
    dot_general x1, matrix products, per_device(): jnp.einsum('ecf,efd->ecd', hidden, w_down, preferred_element_type=jnp.flo...  5.15 us
  transfers between devices with their start and end apart: 3, of which 3 were waited for; matrix products, arithmetic and copies ran while one was open for 1% of the time, Pallas kernels for 0%

profile of v1, /device:TPU:0, one launch (start us, length us, event | category | flops | bytes accessed | tf_op | source)
XLA Modules:
  0.0 168.0 jit_solution(10882180568612723306)
XLA Ops:
  7.2 0.0 copy-start
  7.2 0.0 copy-start.2
  7.2 1.2 copy-done
  8.4 3.3 %fusion.15 = f32[2,64,224]{2,1,0:T(8,128)S(1)} fusion(bf16[2,64,4096]{2,1,0:T(8,128)(2,1)S(1)} %copy-done, bf16[2,4096,224]{1,2,0:T(8,128)(2,1)} %param.12), kind=kOutput, calls=%fused_computation.34 | convolution fusion | flops 234881024 | bytes 4833280 | tf_op jit(solution)/shard_map/ecd,edf->ecf/dot_general | solution.py:136
  11.7 0.0 copy-done.2
  11.7 5.2 %fusion = bf16[2,64,4096]{2,1,0:T(8,128)(2,1)S(1)} fusion(bf16[2,224,4096]{2,1,0:T(8,128)(2,1)} %param.14, bf16[2,64,4096]{2,1,0:T(8,128)(2,1)S(1)} %copy-done, bf16[2,4096,224]{1,2,0:T(8,128)(2,1)} %param.13, f32[2,64]{1,0:T(2,128)S(1)} %copy-done.2, f32[2,64,224]{2,1,0:T(8,128)S(1)} %fusion.15), kind=kOutput, calls=%fused_computation.1 | convolution fusion | flops 470982656 | bytes 9552384 | tf_op jit(solution)/shard_map/ecf,efd->ecd/dot_general | solution.py:142
  16.9 0.0 copy-start.1
  16.9 0.4 copy.17
  17.3 1.3 copy.14
  18.6 5.2 %all-to-all-start = ((bf16[128,8,512]{2,0,1:T(8,128)(2,1)}), bf16[128,8,512]{2,0,1:T(8,128)(2,1)S(1)}, u32[]{:S(2)}, u32[]{:S(2)}) async-start(bf16[128,8,512]{2,0,1:T(8,128)(2,1)} %copy.14), calls=%async_computation | async-start | bytes 2097152 | tf_op jit(solution)/shard_map/all_to_all | solution.py:146
  23.8 0.0 all-gather.5.cloned.1.call-start
  23.8 0.0 copy-done.1
  23.8 0.3 convert_reduce_fusion
  24.2 14.9 %all-to-all-done = bf16[128,8,512]{2,0,1:T(8,128)(2,1)S(1)} async-done(((bf16[128,8,512]{2,0,1:T(8,128)(2,1)}), bf16[128,8,512]{2,0,1:T(8,128)(2,1)S(1)}, u32[]{:S(2)}, u32[]{:S(2)}) %all-to-all-start) | async-done | bytes 1048608 | tf_op jit(solution)/shard_map/all_to_all | solution.py:146
  39.1 0.1 reduce_sum.34
  39.3 0.2 convolution_bitcast_fusion
  39.5 11.9 %all_to_all.18 = bf16[4,64,512]{2,1,0:T(8,128)(2,1)} all-to-all(bf16[4,64,512]{2,1,0:T(8,128)(2,1)S(1)} %bitcast.23), channel_id=1, replica_groups=mesh['expert'=4,'tensor'=8] {'expert'}, dimensions={0} | all-to-all | bytes 524288 | tf_op jit(solution)/shard_map/all_to_all | solution.py:162
  51.4 0.0 all-gather.5.cloned.1.call-update
  51.5 0.0 all-gather.3.cloned.1.call-start
  51.5 0.7 all-gather.3.cloned.1.call-update
  52.2 0.2 select_reduce_fusion
  52.4 0.6 sub.14.slots_ref
  53.1 25.8 %all-gather.5.cloned.1.call-done.rows_ref = bf16[256,4096]{1,0:T(8,128)(2,1)} async-done(((bf16[256,512]{1,0:T(8,128)(2,1)}), bf16[256,4096]{1,0:T(8,128)(2,1)}) %all-gather.5.cloned.1.call-update) | async-done | bytes 2097168 | tf_op jit(solution)/shard_map/all_gather | solution.py:169
  78.9 56.2 %all-gather.3.cloned.1.call-done.residual_ref = bf16[1024,4096]{1,0:T(8,128)(2,1)} async-done(((bf16[128,4096]{1,0:T(8,128)(2,1)}), bf16[1024,4096]{1,0:T(8,128)(2,1)}) %all-gather.3.cloned.1.call-update) | async-done | bytes 8388624 | tf_op jit(solution)/shard_map/all_gather | solution.py:118
  135.0 26.1 %shard_map.104 = (bf16[128,4096]{1,0:T(8,128)(2,1)}, bf16[1024,1536]{1,0:T(8,128)(2,1)}) custom-call(s32[1]{0:T(128)} %bitcast.owner_ref, s32[1,256]{1,0:T(1,128)} %sub.14.slots_ref, bf16[1024,4096]{1,0:T(8,128)(2,1)} %all-gather.3.cloned.1.call-done.residual_ref, bf16[256,4096]{1,0:T(8,128)(2,1)} %all-gather.5.cloned.1.call-done.rows_ref, ...), custom_call_target="tpu_custom_call" | custom-call | flops 15032385536 | bytes 15728640 | tf_op jit(solution)/shard_map/pallas_call | solution.py:73
  (8 shorter events, 0.1 us)
Async XLA Ops:
  7.2 1.2 copy-start
  7.2 4.5 %copy-start.2 = (f32[2,64]{1,0:T(2,128)S(1)}, f32[2,64]{1,0:T(2,128)}, u32[]{:S(2)}) copy-start(f32[2,64]{1,0:T(2,128)} %param.10) | copy-start | bytes 1540
  16.9 7.0 %copy-start.1 = (s32[8,64]{1,0:T(8,128)S(1)}, s32[8,64]{1,0:T(8,128)}, u32[]{:S(2)}) copy-start(s32[8,64]{1,0:T(8,128)} %param.11) | copy-start | bytes 6148
  18.6 20.6 %all-to-all-start = ((bf16[128,8,512]{2,0,1:T(8,128)(2,1)}), bf16[128,8,512]{2,0,1:T(8,128)(2,1)S(1)}, u32[]{:S(2)}, u32[]{:S(2)}) async-start(bf16[128,8,512]{2,0,1:T(8,128)(2,1)} %copy.14), calls=%async_computation | async-start | bytes 2097152 | tf_op jit(solution)/shard_map/all_to_all | solution.py:146
  23.8 55.1 %all-gather.5.cloned.1.call-start = ((), (), s32[]{:S(2)}) async-start(), calls=%async_computation.3 | async-start | bytes 2359296 | tf_op jit(solution)/shard_map/all_gather | solution.py:169
  51.5 83.6 %all-gather.3.cloned.1.call-start = ((), (), s32[]{:S(2)}) async-start(), calls=%async_computation.2 | async-start | bytes 9437184 | tf_op jit(solution)/shard_map/all_gather | solution.py:118
Sparse Core Ops, SparseCore 0:
  51.6 27.2 all-gather.4
  80.7 54.2 all-gather.2

commit v2 on v1

--- a/solution.py
+++ b/solution.py
@@ -8,10 +8,12 @@
 from jax.sharding import PartitionSpec as P
 
 MOST = 4
+MESH = pl.DeviceIdType.MESH
 
 
 def finish_kernel(
     row_steps,
+    order,
     owner_ref,
     slots_ref,
     residual_ref,
@@ -25,7 +27,7 @@
 ):
     step = pl.program_id(0)
     tok_rows, feature_width = residual_ref.shape
-    chunk = 512
+    chunk = rows_ref.shape[2]
 
     @pl.when(step < row_steps)
     def _():
@@ -34,10 +36,10 @@
             jnp.bfloat16
         )
         squares = jnp.zeros((tok_rows, 128), jnp.float32)
-        for start in range(0, feature_width, chunk):
+        for place, start in enumerate(range(0, feature_width, chunk)):
             cols = pl.ds(start, chunk)
             combined = residual_ref[:, cols].astype(jnp.float32) + jnp.dot(
-                placement, rows_ref[:, cols], preferred_element_type=jnp.float32
+                placement, rows_ref[order[place]], preferred_element_type=jnp.float32
             )
             combined_ref[:, cols] = combined
             for part in range(0, chunk, 128):
@@ -63,21 +65,21 @@
         ).astype(jnp.bfloat16)
 
 
-def finish(owner, slots, residual_all, rows, gain, w_qkv, tok_rows):
+def finish(owner, slots, residual_all, rows, order, gain, w_qkv, tok_rows):
     total_rows, feature_width = residual_all.shape
     columns = w_qkv.shape[1]
     tile = 256
     row_steps = total_rows // tok_rows
     col_steps = columns // tile
-    slot_total = rows.shape[0]
+    slot_total = rows.shape[1]
     return pl.pallas_call(
-        functools.partial(finish_kernel, row_steps),
+        functools.partial(finish_kernel, row_steps, order),
         grid=(row_steps + col_steps,),
         in_specs=[
             pl.BlockSpec(memory_space=pltpu.SMEM),
             pl.BlockSpec((1, slot_total), lambda i: (0, 0)),
             pl.BlockSpec((tok_rows, feature_width), lambda i: (jnp.minimum(i, row_steps - 1), 0)),
-            pl.BlockSpec((slot_total, feature_width), lambda i: (0, 0)),
+            pl.BlockSpec(rows.shape, lambda i: (0, 0, 0)),
             pl.BlockSpec((1, feature_width), lambda i: (0, 0)),
             pl.BlockSpec((feature_width, tile), lambda i: (0, jnp.maximum(i - row_steps, 0))),
         ],
@@ -104,35 +106,285 @@
     )(owner, slots, residual_all, rows, gain, w_qkv)
 
 
-def per_device(
-    expert_inputs, gates, chosen_tokens, w_gate, w_up, w_down, residual, norm_gain, w_qkv
+def comm_kernel(
+    groups,
+    inputs_ref,
+    gates_ref,
+    table_ref,
+    gate_hbm,
+    up_hbm,
+    down_hbm,
+    residual_hbm,
+    blocks_out,
+    rows_out,
+    gate_w,
+    up_w,
+    down_w,
+    own,
+    partial,
+    half_in,
+    chips_sum,
+    chips_in,
+    outgoing,
+    slots_in,
+    load_sem,
+    first_send,
+    first_recv,
+    reduce_send,
+    reduce_recv,
+    group_send,
+    group_recv,
+    block_send,
+    block_recv,
+    row_send,
+    row_recv,
+    keep_sem,
 ):
-    expert_count = lax.axis_size("expert")
-    tensor_count = lax.axis_size("tensor")
-    my_group = lax.axis_index("expert")
+    group = lax.axis_index("expert")
+    me = lax.axis_index("tensor")
+    core = me % 2
+    partner = me + 1 - 2 * core
+    along_x = me + 2 - 4 * ((me // 2) % 2)
+    along_y = me + 4 - 8 * (me // 4)
+    across = along_x + 4 - 8 * (me // 4)
+    local_experts, slot_count, feature_width = inputs_ref.shape
+    chips, row_total, width = chips_sum.shape
+
+    def send(source, target, send_sem, recv_sem, device):
+        copy = pltpu.make_async_remote_copy(
+            src_ref=source,
+            dst_ref=target,
+            send_sem=send_sem,
+            recv_sem=recv_sem,
+            device_id=device,
+            device_id_type=MESH,
+        )
+        copy.start()
+        return copy
+
+    loads = [pltpu.make_async_copy(residual_hbm, own, load_sem.at[0])]
+    for index, (hbm, vmem) in enumerate(((gate_hbm, gate_w), (up_hbm, up_w), (down_hbm, down_w))):
+        loads.append(pltpu.make_async_copy(hbm, vmem, load_sem.at[index + 1]))
+    for copy in loads:
+        copy.start()
+
+    barrier = pltpu.get_barrier_semaphore()
+    peers = [(group, device) for device in (partner, along_x, along_y, across)]
+    peers += [((group + d) % groups, me) for d in range(1, groups)]
+    for device in peers:
+        pl.semaphore_signal(barrier, inc=1, device_id=device, device_id_type=MESH)
+    pl.semaphore_wait(barrier, len(peers))
+
+    def gather_parts(source, target, send_sem, recv_sem):
+        half = source.shape[0] // 2
+        parts = (pl.ds(0, half), pl.ds(half, half))
+
+        def direct(which, device):
+            role = 0 if device is along_x else 2
+            return send(
+                source.at[parts[which]],
+                target.at[me, parts[which]],
+                send_sem.at[role + which],
+                recv_sem.at[role + which],
+                (group, device),
+            )
+
+        def onward(which):
+            origin, device = ((along_x, along_y), (along_y, along_x))[which]
+            return send(
+                target.at[origin, parts[which]],
+                target.at[origin, parts[which]],
+                send_sem.at[4 + which],
+                recv_sem.at[4 + which],
+                (group, device),
+            )
+
+        def to_partner(role, block):
+            return send(
+                block,
+                target.at[(me, along_x, along_y, across)[role]],
+                send_sem.at[6 + role],
+                recv_sem.at[6 + role],
+                (group, partner),
+            )
+
+        return direct, onward, to_partner
+
+    block_direct, block_onward, block_partner = gather_parts(
+        own, blocks_out, block_send, block_recv
+    )
+    row_direct, row_onward, row_partner = gather_parts(slots_in, rows_out, row_send, row_recv)
+
+    loads[0].wait()
+    block_x0 = block_direct(0, along_x)
+    block_y1 = block_direct(1, along_y)
+    block_own = block_partner(0, own)
+    keep_block = pltpu.make_async_copy(own, blocks_out.at[me], keep_sem.at[0])
+    keep_block.start()
+
+    for copy in loads[1:]:
+        copy.wait()
+    contract = (((1,), (1,)), ((), ()))
+    for expert in range(local_experts):
+        gate_part = lax.dot_general(
+            inputs_ref[expert], gate_w[expert], contract, preferred_element_type=jnp.float32
+        )
+        up_part = lax.dot_general(
+            inputs_ref[expert], up_w[expert], contract, preferred_element_type=jnp.float32
+        )
+        hidden = (gate_part / (1.0 + jnp.exp(-gate_part)) * up_part).astype(jnp.bfloat16)
+        lines = pl.ds(expert * slot_count, slot_count)
+        for place in range(2 * chips):
+            value = jnp.dot(
+                hidden,
+                down_w[expert, :, place * width : (place + 1) * width],
+                preferred_element_type=jnp.float32,
+            )
+            partial[place, lines, :] = (value * gates_ref[expert]).astype(jnp.bfloat16)
+
+    first = send(
+        partial.at[pl.ds((1 - core) * chips, chips)],
+        half_in,
+        first_send,
+        first_recv,
+        (group, partner),
+    )
+    first.wait_recv()
+    for chip in range(chips):
+        chips_sum[chip] = (
+            partial[core * chips + chip].astype(jnp.float32) + half_in[chip].astype(jnp.float32)
+        ).astype(jnp.bfloat16)
+    reduces = [
+        send(
+            chips_sum.at[device // 2],
+            chips_in.at[index],
+            reduce_send.at[index],
+            reduce_recv.at[index],
+            (group, device),
+        )
+        for index, device in enumerate((across, along_x, along_y))
+    ]
+    block_x1 = block_direct(1, along_x)
+    block_y0 = block_direct(0, along_y)
+    for copy in reduces:
+        copy.wait_recv()
+    total = chips_sum[me // 2].astype(jnp.float32)
+    for index in range(3):
+        total = total + chips_in[index].astype(jnp.float32)
+    total = total.astype(jnp.bfloat16)
+    for place in range(groups):
+        outgoing[place] = jnp.dot(
+            table_ref[place], total, preferred_element_type=jnp.float32
+        ).astype(jnp.bfloat16)
+    exchanges = [
+        send(
+            outgoing.at[(group + d) % groups],
+            slots_in.at[group],
+            group_send.at[d - 1],
+            group_recv.at[d - 1],
+            ((group + d) % groups, me),
+        )
+        for d in range(1, groups)
+    ]
+    slots_in[group] = outgoing[group]
+    block_x0.wait_recv()
+    block_o0 = block_onward(0)
+    block_y1.wait_recv()
+    block_o1 = block_onward(1)
+    for copy in exchanges:
+        copy.wait_recv()
+    row_x0 = row_direct(0, along_x)
+    row_y1 = row_direct(1, along_y)
+    row_x1 = row_direct(1, along_x)
+    row_y0 = row_direct(0, along_y)
+    row_own = row_partner(0, slots_in)
+    keep_rows = pltpu.make_async_copy(slots_in, rows_out.at[me], keep_sem.at[1])
+    keep_rows.start()
+
+    block_x1.wait_recv()
+    block_px = block_partner(1, blocks_out.at[along_x])
+    block_y0.wait_recv()
+    block_py = block_partner(2, blocks_out.at[along_y])
+    row_x0.wait_recv()
+    row_o0 = row_onward(0)
+    row_y1.wait_recv()
+    row_o1 = row_onward(1)
+    block_o0.wait_recv()
+    block_o1.wait_recv()
+    block_pd = block_partner(3, blocks_out.at[across])
+    row_x1.wait_recv()
+    row_px = row_partner(1, rows_out.at[along_x])
+    row_y0.wait_recv()
+    row_py = row_partner(2, rows_out.at[along_y])
+    row_o0.wait_recv()
+    row_o1.wait_recv()
+    row_pd = row_partner(3, rows_out.at[across])
+
+    keep_block.wait()
+    keep_rows.wait()
+    last = [block_own, block_px, block_py, block_pd, row_own, row_px, row_py, row_pd]
+    for copy in last:
+        copy.wait_recv()
+    sent = last + reduces + exchanges + [first, block_x0, block_x1, block_y0, block_y1, block_o0]
+    sent += [block_o1, row_x0, row_x1, row_y0, row_y1, row_o0, row_o1]
+    for copy in sent:
+        copy.wait_send()
+
+
+def communicate(groups, members, table, inputs, gates, w_gate, w_up, w_down, residual):
+    local_experts, slot_count, feature_width = inputs.shape
+    tok_rows = residual.shape[0]
+    row_total = local_experts * slot_count
+    width = feature_width // members
+    chips = members // 2
+    keep = table.shape[1]
+    bf16 = jnp.bfloat16
+    anywhere = pl.BlockSpec(memory_space=pl.ANY)
+    vmem = pl.BlockSpec(memory_space=pltpu.VMEM)
+    dma = pltpu.SemaphoreType.DMA
+    gate_t, up_t = jnp.swapaxes(w_gate, 1, 2), jnp.swapaxes(w_up, 1, 2)
+    return pl.pallas_call(
+        functools.partial(comm_kernel, groups),
+        in_specs=[vmem, vmem, vmem, anywhere, anywhere, anywhere, anywhere],
+        out_specs=[anywhere, anywhere],
+        out_shape=[
+            jax.ShapeDtypeStruct((members, tok_rows, feature_width), bf16),
+            jax.ShapeDtypeStruct((members, groups, keep, width), bf16),
+        ],
+        scratch_shapes=[
+            pltpu.VMEM(gate_t.shape, bf16),
+            pltpu.VMEM(up_t.shape, bf16),
+            pltpu.VMEM(w_down.shape, bf16),
+            pltpu.VMEM((tok_rows, feature_width), bf16),
+            pltpu.VMEM((members, row_total, width), bf16),
+            pltpu.VMEM((chips, row_total, width), bf16),
+            pltpu.VMEM((chips, row_total, width), bf16),
+            pltpu.VMEM((chips - 1, row_total, width), bf16),
+            pltpu.VMEM((groups, keep, width), bf16),
+            pltpu.VMEM((groups, keep, width), bf16),
+            dma((4,)),
+            dma,
+            dma,
+            dma((3,)),
+            dma((3,)),
+            dma((groups - 1,)),
+            dma((groups - 1,)),
+            dma((10,)),
+            dma((10,)),
+            dma((10,)),
+            dma((10,)),
+            dma((2,)),
+        ],
+        compiler_params=pltpu.CompilerParams(
+            collective_id=0, has_side_effects=True, vmem_limit_bytes=60 * 1024 * 1024
+        ),
+    )(inputs, gates[:, :, None], table, gate_t, up_t, w_down, residual)
+
+
+def plain_rows(
+    expert_inputs, gates, w_gate, w_up, w_down, send_table, expert_count, tensor_count
+):
     local_experts, slot_count, feature_width = expert_inputs.shape
-    tok_rows = residual.shape[0]
-    group_rows = tok_rows * tensor_count
-    keep = min(slot_count, MOST * tensor_count)
-
-    residual_all = lax.all_gather(residual, "tensor", axis=0, tiled=True)
-
-    dest = chosen_tokens // group_rows
-    earlier = jnp.arange(slot_count)[None, :] < jnp.arange(slot_count)[:, None]
-    rank = jnp.sum(
-        ((dest[:, :, None] == dest[:, None, :]) & earlier[None]).astype(jnp.int32), axis=2
-    )
-    kept = jnp.arange(keep, dtype=jnp.int32)
-    mine = jnp.where(dest == my_group, rank, -1)
-    token_at = jnp.sum(
-        jnp.where(
-            mine[:, None, :] == kept[None, :, None],
-            (chosen_tokens % group_rows)[:, None, :] + 1,
-            0,
-        ),
-        axis=2,
-    ).reshape(1, -1) - 1
-
     gate_part = jnp.einsum(
         "ecd,edf->ecf", expert_inputs, w_gate, preferred_element_type=jnp.float32
     )
@@ -152,27 +404,82 @@
     ).reshape(tensor_count, local_experts, slot_count, -1)
     summed = jnp.sum(arrived.astype(jnp.float32), axis=0).astype(jnp.bfloat16)
 
+    outgoing = jnp.einsum("zlkmj,mjf->zlkf", send_table, summed)
+    incoming = lax.all_to_all(
+        outgoing.reshape(expert_count, -1, outgoing.shape[-1]),
+        "expert",
+        split_axis=0,
+        concat_axis=0,
+        tiled=True,
+    )
+    incoming = incoming.reshape(-1, outgoing.shape[-1])
+    return lax.all_gather(incoming, "tensor", axis=0, tiled=False)
+
+
+def per_device(
+    expert_inputs, gates, chosen_tokens, w_gate, w_up, w_down, residual, norm_gain, w_qkv
+):
+    expert_count = lax.axis_size("expert")
+    tensor_count = lax.axis_size("tensor")
+    my_group = lax.axis_index("expert")
+    local_experts, slot_count, feature_width = expert_inputs.shape
+    tok_rows = residual.shape[0]
+    group_rows = tok_rows * tensor_count
+    keep = min(slot_count, MOST * tensor_count)
+
+    dest = chosen_tokens // group_rows
+    earlier = jnp.arange(slot_count)[None, :] < jnp.arange(slot_count)[:, None]
+    rank = jnp.sum(
+        ((dest[:, :, None] == dest[:, None, :]) & earlier[None]).astype(jnp.int32), axis=2
+    )
+    kept = jnp.arange(keep, dtype=jnp.int32)
+    mine = jnp.where(dest == my_group, rank, -1)
+    token_at = jnp.sum(
+        jnp.where(
+            mine[:, None, :] == kept[None, :, None],
+            (chosen_tokens % group_rows)[:, None, :] + 1,
+            0,
+        ),
+        axis=2,
+    ).reshape(1, -1) - 1
+
     local_dest = lax.dynamic_slice_in_dim(dest, my_group * local_experts, local_experts, 0)
     local_rank = lax.dynamic_slice_in_dim(rank, my_group * local_experts, local_experts, 0)
     send_table = (
         (local_dest[None, :, None, :] == jnp.arange(expert_count)[:, None, None, None])
         & (local_rank[None, :, None, :] == kept[None, None, :, None])
     ).astype(jnp.bfloat16)
-    outgoing = jnp.einsum("zlkj,ljf->zlkf", send_table, summed)
-    incoming = lax.all_to_all(
-        outgoing.reshape(expert_count, local_experts * keep, -1),
-        "expert",
-        split_axis=0,
-        concat_axis=0,
-        tiled=True,
-    ).reshape(expert_count * local_experts * keep, -1)
-    rows = lax.all_gather(incoming, "tensor", axis=1, tiled=True)
+    same = jnp.eye(local_experts, dtype=jnp.bfloat16)
+    send_table = send_table[:, :, :, None, :] * same[None, :, None, :, None]
+    if tensor_count == 8:
+        residual_all, rows = communicate(
+            expert_count,
+            tensor_count,
+            send_table.reshape(expert_count, local_experts * keep, -1),
+            expert_inputs,
+            gates,
+            w_gate,
+            w_up,
+            w_down,
+            residual,
+        )
+        residual_all = residual_all.reshape(group_rows, feature_width)
+        rows = rows.reshape(tensor_count, -1, feature_width // tensor_count)
+        chips = tensor_count // 2
+        order = tuple((c % chips) * 2 + c // chips for c in range(tensor_count))
+    else:
+        residual_all = lax.all_gather(residual, "tensor", axis=0, tiled=True)
+        rows = plain_rows(
+            expert_inputs, gates, w_gate, w_up, w_down, send_table, expert_count, tensor_count
+        )
+        order = tuple(range(tensor_count))
 
     return finish(
         lax.axis_index("tensor").reshape(1),
         token_at,
         residual_all,
         rows,
+        order,
         norm_gain[None, :],
         w_qkv,
         tok_rows,

time: 168 us -> 90.3 us (0.54)
  waiting for transfers between devices: 97.6 us -> 0 us
  Pallas kernels: 26.1 us -> 84.2 us
  between operations: 14.2 us -> 0.72 us
  blocking collectives: 11.9 us -> 0 us
  matrix products: 8.65 us -> 0 us
  starting transfers between devices: 5.28 us -> 0 us
  other arithmetic: 0.73 us -> 2.62 us
    all_gather x2 -> x0, waiting for transfers between devices: 82 us -> none  [the longest x1 56.2 us: per_device(): residual_all = lax.all_gather(residual, 'tensor', axis=0, tiled=True)]
    pallas_call x1 -> x2, Pallas kernels: 26.1 us -> 84.2 us  [the longest x1 58.5 us: communicate(): pl.pallas_call(functools.partial(comm_kernel, groups), in_specs=[vmem, vm...]
    all_to_all x1 -> x0, waiting for transfers between devices: 14.9 us -> none  [per_device(): lax.all_to_all(partial_value.reshape(row_total, feature_width), 'tensor',...]
    all_to_all x1 -> x0, blocking collectives: 11.9 us -> none  [per_device(): lax.all_to_all(outgoing.reshape(expert_count, local_experts * keep, -1),...]
    dot_general x3 -> x0, matrix products: 8.65 us -> none  [the longest x1 5.15 us: per_device(): jnp.einsum('ecf,efd->ecd', hidden, w_down, preferred_element_type=jnp.flo...]
    all_to_all x1 -> x0, starting transfers between devices: 5.2 us -> none  [per_device(): lax.all_to_all(partial_value.reshape(row_total, feature_width), 'tensor',...]
  transfers between devices with their start and end apart: 3 -> 0, of which waited for: 3 -> 0; matrix products, arithmetic and copies ran while one was open for 1% -> 0% of each run, Pallas kernels for 0% -> 0%
where the time goes in v2:
time: 90.3 us; the launch traced here: 90 us
  Pallas kernels  84.2 us (93%)
  other arithmetic  2.62 us (3%)
  local copies, waits for them, and re-layouts  2.45 us (3%)
    pallas_call x1, Pallas kernels, communicate(): pl.pallas_call(functools.partial(comm_kernel, groups), in_specs=[vmem, vm...  58.5 us
    pallas_call x1, Pallas kernels, finish(): pl.pallas_call(functools.partial(finish_kernel, row_steps, order), grid=(...  25.7 us

profile of v2, /device:TPU:0, one launch (start us, length us, event | category | flops | bytes accessed | tf_op | source)
XLA Modules:
  0.0 90.0 jit_solution(1745551080445907502)
XLA Ops:
  0.6 0.7 add_select_fusion.1
  1.4 0.3 convert_reduce_fusion
  1.7 0.7 compare_select_fusion
  2.4 0.2 select_reduce_fusion
  2.6 0.7 sub.14.slots_ref
  3.3 0.1 mul.27
  3.4 0.1 mul.28
  3.5 0.1 mul.25
  3.6 0.1 mul.26
  3.7 0.6 broadcast_multiply_fusion.table_ref
  4.4 1.4 %copy.12.gates_ref = f32[2,64,1]{2,1,0:T(8,128)} copy(f32[2,64,1]{1,0,2:T(2,128)} %bitcast.9) | data formatting | bytes 1024 | tf_op jit(solution)/shard_map/broadcast_in_dim | solution.py:381
  5.8 58.5 %shard_map.104 = (bf16[8,128,4096]{2,1,0:T(8,128)(2,1)}, bf16[8,4,64,512]{3,2,1,0:T(8,128)(2,1)}) custom-call(bf16[2,64,4096]{2,1,0:T(8,128)(2,1)} %inputs_ref.1, f32[2,64,1]{2,1,0:T(8,128)} %copy.12.gates_ref, bf16[4,64,128]{2,1,0:T(8,128)(2,1)} %broadcast_multiply_fusion.table_ref, bf16[2,224,4096]{2,1,0:T(8,128)(2,1)} %bitcast.7, ...), custom_call_target="tpu_custom_call" | custom-call | tf_op jit(solution)/shard_map/pallas_call | solution.py:346
  64.2 25.7 %shard_map.105 = (bf16[128,4096]{1,0:T(8,128)(2,1)}, bf16[1024,1536]{1,0:T(8,128)(2,1)}) custom-call(s32[1]{0:T(128)} %bitcast.owner_ref, s32[1,256]{1,0:T(1,128)} %sub.14.slots_ref, bf16[1024,4096]{1,0:T(8,128)(2,1)} %bitcast.10, bf16[8,256,512]{2,1,0:T(8,128)(2,1)} %bitcast.11, f32[1,4096]{1,0:T(1,128)} %bitcast.12, bf16[4096,1536]{1,0:T(8,128)(2,1)} %weight_ref.1), custom_call_target="tpu_custom_call" | custom-call | flops 15032385536 | bytes 15728640 | tf_op jit(solution)/shard_map/pallas_call | solution.py:75
  (7 shorter events, 0.1 us)

commit v3 on v2

--- a/solution.py
+++ b/solution.py
@@ -115,18 +115,25 @@
     up_hbm,
     down_hbm,
     residual_hbm,
-    blocks_out,
-    rows_out,
+    slots_ref,
+    gain_ref,
+    weight_hbm,
+    stream_ref,
+    projected_hbm,
     gate_w,
     up_w,
     down_w,
-    own,
+    weight,
+    blocks,
+    rows,
+    combined_ref,
+    normed_ref,
+    staged,
     partial,
     half_in,
     chips_sum,
     chips_in,
     outgoing,
-    slots_in,
     load_sem,
     first_send,
     first_recv,
@@ -138,7 +145,7 @@
     block_recv,
     row_send,
     row_recv,
-    keep_sem,
+    store_sem,
 ):
     group = lax.axis_index("expert")
     me = lax.axis_index("tensor")
@@ -162,11 +169,14 @@
         copy.start()
         return copy
 
-    loads = [pltpu.make_async_copy(residual_hbm, own, load_sem.at[0])]
+    tok_rows = residual_hbm.shape[0]
+    loads = [pltpu.make_async_copy(residual_hbm, blocks.at[me], load_sem.at[0])]
     for index, (hbm, vmem) in enumerate(((gate_hbm, gate_w), (up_hbm, up_w), (down_hbm, down_w))):
         loads.append(pltpu.make_async_copy(hbm, vmem, load_sem.at[index + 1]))
     for copy in loads:
         copy.start()
+    load_weight = pltpu.make_async_copy(weight_hbm, weight, load_sem.at[4])
+    load_weight.start()
 
     barrier = pltpu.get_barrier_semaphore()
     peers = [(group, device) for device in (partner, along_x, along_y, across)]
@@ -175,52 +185,27 @@
         pl.semaphore_signal(barrier, inc=1, device_id=device, device_id_type=MESH)
     pl.semaphore_wait(barrier, len(peers))
 
-    def gather_parts(source, target, send_sem, recv_sem):
-        half = source.shape[0] // 2
-        parts = (pl.ds(0, half), pl.ds(half, half))
-
-        def direct(which, device):
-            role = 0 if device is along_x else 2
-            return send(
-                source.at[parts[which]],
-                target.at[me, parts[which]],
-                send_sem.at[role + which],
-                recv_sem.at[role + which],
-                (group, device),
-            )
-
-        def onward(which):
-            origin, device = ((along_x, along_y), (along_y, along_x))[which]
-            return send(
-                target.at[origin, parts[which]],
-                target.at[origin, parts[which]],
-                send_sem.at[4 + which],
-                recv_sem.at[4 + which],
-                (group, device),
-            )
-
-        def to_partner(role, block):
-            return send(
-                block,
-                target.at[(me, along_x, along_y, across)[role]],
-                send_sem.at[6 + role],
-                recv_sem.at[6 + role],
-                (group, partner),
-            )
-
-        return direct, onward, to_partner
-
-    block_direct, block_onward, block_partner = gather_parts(
-        own, blocks_out, block_send, block_recv
-    )
-    row_direct, row_onward, row_partner = gather_parts(slots_in, rows_out, row_send, row_recv)
+    half, quarter, groups_half = tok_rows // 2, tok_rows // 4, groups // 2
+    corner = (me, along_x, along_y, across)
+
+    def block_send_to(index, origin, start, size, device):
+        part = blocks.at[origin, pl.ds(start, size)]
+        return send(part, part, block_send.at[index], block_recv.at[index], (group, device))
+
+    def row_send_to(index, origin, start, size, device):
+        part = rows.at[origin, pl.ds(start, size)]
+        return send(part, part, row_send.at[index], row_recv.at[index], (group, device))
+
+    def block_partner(role):
+        return block_send_to(8 + role, corner[role], 0, tok_rows, partner)
+
+    def row_partner(role):
+        return row_send_to(6 + role, corner[role], 0, groups, partner)
 
     loads[0].wait()
-    block_x0 = block_direct(0, along_x)
-    block_y1 = block_direct(1, along_y)
-    block_own = block_partner(0, own)
-    keep_block = pltpu.make_async_copy(own, blocks_out.at[me], keep_sem.at[0])
-    keep_block.start()
+    block_x0 = block_send_to(0, me, 0, half, along_x)
+    block_y0 = block_send_to(1, me, half, half, along_y)
+    block_own = block_partner(0)
 
     for copy in loads[1:]:
         copy.wait()
@@ -264,8 +249,8 @@
         )
         for index, device in enumerate((across, along_x, along_y))
     ]
-    block_x1 = block_direct(1, along_x)
-    block_y0 = block_direct(0, along_y)
+    block_x1 = block_send_to(2, me, half, quarter, along_x)
+    block_y1 = block_send_to(3, me, 0, quarter, along_y)
     for copy in reduces:
         copy.wait_recv()
     total = chips_sum[me // 2].astype(jnp.float32)
@@ -279,59 +264,127 @@
     exchanges = [
         send(
             outgoing.at[(group + d) % groups],
-            slots_in.at[group],
+            rows.at[me, group],
             group_send.at[d - 1],
             group_recv.at[d - 1],
             ((group + d) % groups, me),
         )
         for d in range(1, groups)
     ]
-    slots_in[group] = outgoing[group]
-    block_x0.wait_recv()
-    block_o0 = block_onward(0)
-    block_y1.wait_recv()
-    block_o1 = block_onward(1)
+    rows[me, group] = outgoing[group]
     for copy in exchanges:
         copy.wait_recv()
-    row_x0 = row_direct(0, along_x)
-    row_y1 = row_direct(1, along_y)
-    row_x1 = row_direct(1, along_x)
-    row_y0 = row_direct(0, along_y)
-    row_own = row_partner(0, slots_in)
-    keep_rows = pltpu.make_async_copy(slots_in, rows_out.at[me], keep_sem.at[1])
-    keep_rows.start()
-
+    rest = groups - groups_half
+    row_x0 = row_send_to(0, me, 0, groups_half, along_x)
+    row_y0 = row_send_to(1, me, groups_half, rest, along_y)
+    row_x1 = row_send_to(2, me, groups_half, rest, along_x)
+    row_y1 = row_send_to(3, me, 0, groups_half, along_y)
+    row_own = row_partner(0)
+    row_x0.wait_recv()
+    row_ox = row_send_to(4, along_x, 0, groups_half, along_y)
+    row_y0.wait_recv()
+    row_oy = row_send_to(5, along_y, groups_half, rest, along_x)
+    block_x2 = block_send_to(4, me, half + quarter, quarter, along_x)
+    block_y2 = block_send_to(5, me, quarter, quarter, along_y)
+    block_x0.wait_recv()
+    block_ox = block_send_to(6, along_x, 0, half, along_y)
+    block_y0.wait_recv()
+    block_oy = block_send_to(7, along_y, half, half, along_x)
+    row_x1.wait_recv()
+    row_px = row_partner(1)
+    row_y1.wait_recv()
+    row_py = row_partner(2)
+    row_ox.wait_recv()
+    row_oy.wait_recv()
+    row_pd = row_partner(3)
+    block_own.wait_recv()
+    for copy in (row_own, row_px, row_py, row_pd):
+        copy.wait_recv()
+    load_weight.wait()
+
+    pair = 2 * tok_rows
+    slot_total = slots_ref.shape[1]
+    tile = 256
+    col_tiles = weight.shape[1] // tile
+    stores = []
+
+    def finish_pair(step, chip):
+        def place(index, squares):
+            cols = pl.ds(pl.multiple_of(index * width, width), width)
+            tokens = lax.broadcasted_iota(jnp.int32, (pair, slot_total), 0) + chip * pair
+            placement = jnp.where(slots_ref[...] == tokens, 1.0, 0.0).astype(jnp.bfloat16)
+            source = (index % chips) * 2 + index // chips
+            values = rows[source].reshape(slot_total, width)
+            block = blocks[pl.ds(2 * chip, 2), :, cols].reshape(pair, width)
+            combined = block.astype(jnp.float32) + jnp.dot(
+                placement, values, preferred_element_type=jnp.float32
+            )
+            combined_ref[:, cols] = combined
+            for part in range(0, width, 128):
+                piece = combined[:, part : part + 128]
+                squares = squares + piece * piece
+            return squares
+
+        squares = lax.fori_loop(0, 2 * chips, place, jnp.zeros((pair, 128), jnp.float32))
+        scale = lax.rsqrt(jnp.sum(squares, axis=1, keepdims=True) / feature_width + 1e-06)
+
+        def norm(index, carry):
+            cols = pl.ds(pl.multiple_of(index * width, width), width)
+            normed_ref[:, cols] = (combined_ref[:, cols] * scale * gain_ref[:, cols]).astype(
+                jnp.bfloat16
+            )
+            return carry
+
+        lax.fori_loop(0, 2 * chips, norm, 0)
+        if step == 0:
+            begin = pl.multiple_of(core * tok_rows, tok_rows)
+            stream_ref[...] = combined_ref[pl.ds(begin, tok_rows), :].astype(jnp.bfloat16)
+
+        def project(index, carry):
+            cols = pl.ds(pl.multiple_of(index * tile, tile), tile)
+            staged[step, :, cols] = jnp.dot(
+                normed_ref[...], weight[:, cols], preferred_element_type=jnp.float32
+            ).astype(jnp.bfloat16)
+            return carry
+
+        lax.fori_loop(0, col_tiles, project, 0)
+        begin = pl.multiple_of(chip * pair, pair)
+        store = pltpu.make_async_copy(
+            staged.at[step], projected_hbm.at[pl.ds(begin, pair)], store_sem.at[step]
+        )
+        store.start()
+        stores.append(store)
+
+    finish_pair(0, me // 2)
     block_x1.wait_recv()
-    block_px = block_partner(1, blocks_out.at[along_x])
-    block_y0.wait_recv()
-    block_py = block_partner(2, blocks_out.at[along_y])
-    row_x0.wait_recv()
-    row_o0 = row_onward(0)
-    row_y1.wait_recv()
-    row_o1 = row_onward(1)
-    block_o0.wait_recv()
-    block_o1.wait_recv()
-    block_pd = block_partner(3, blocks_out.at[across])
-    row_x1.wait_recv()
-    row_px = row_partner(1, rows_out.at[along_x])
-    row_y0.wait_recv()
-    row_py = row_partner(2, rows_out.at[along_y])
-    row_o0.wait_recv()
-    row_o1.wait_recv()
-    row_pd = row_partner(3, rows_out.at[across])
-
-    keep_block.wait()
-    keep_rows.wait()
-    last = [block_own, block_px, block_py, block_pd, row_own, row_px, row_py, row_pd]
-    for copy in last:
-        copy.wait_recv()
-    sent = last + reduces + exchanges + [first, block_x0, block_x1, block_y0, block_y1, block_o0]
-    sent += [block_o1, row_x0, row_x1, row_y0, row_y1, row_o0, row_o1]
+    block_x2.wait_recv()
+    block_px = block_partner(1)
+    block_y1.wait_recv()
+    block_y2.wait_recv()
+    block_py = block_partner(2)
+    block_px.wait_recv()
+    finish_pair(1, along_x // 2)
+    block_ox.wait_recv()
+    block_oy.wait_recv()
+    block_pd = block_partner(3)
+    block_py.wait_recv()
+    finish_pair(2, along_y // 2)
+    block_pd.wait_recv()
+    finish_pair(3, across // 2)
+
+    sent = [block_own, block_px, block_py, block_pd, row_own, row_px, row_py, row_pd]
+    sent += reduces + exchanges + [first, block_x0, block_x1, block_x2]
+    sent += [block_y0, block_y1, block_y2, block_ox, block_oy]
+    sent += [row_x0, row_x1, row_y0, row_y1, row_ox, row_oy]
     for copy in sent:
         copy.wait_send()
-
-
-def communicate(groups, members, table, inputs, gates, w_gate, w_up, w_down, residual):
+    for store in stores:
+        store.wait()
+
+
+def communicate(
+    groups, members, table, inputs, gates, w_gate, w_up, w_down, residual, slots, gain, w_qkv
+):
     local_experts, slot_count, feature_width = inputs.shape
     tok_rows = residual.shape[0]
     row_total = local_experts * slot_count
@@ -345,40 +398,44 @@
     gate_t, up_t = jnp.swapaxes(w_gate, 1, 2), jnp.swapaxes(w_up, 1, 2)
     return pl.pallas_call(
         functools.partial(comm_kernel, groups),
-        in_specs=[vmem, vmem, vmem, anywhere, anywhere, anywhere, anywhere],
-        out_specs=[anywhere, anywhere],
+        in_specs=[vmem] * 3 + [anywhere] * 4 + [vmem, vmem, anywhere],
+        out_specs=[vmem, anywhere],
         out_shape=[
-            jax.ShapeDtypeStruct((members, tok_rows, feature_width), bf16),
-            jax.ShapeDtypeStruct((members, groups, keep, width), bf16),
+            jax.ShapeDtypeStruct((tok_rows, feature_width), bf16),
+            jax.ShapeDtypeStruct((members * tok_rows, w_qkv.shape[1]), bf16),
         ],
         scratch_shapes=[
             pltpu.VMEM(gate_t.shape, bf16),
             pltpu.VMEM(up_t.shape, bf16),
             pltpu.VMEM(w_down.shape, bf16),
-            pltpu.VMEM((tok_rows, feature_width), bf16),
+            pltpu.VMEM(w_qkv.shape, bf16),
+            pltpu.VMEM((members, tok_rows, feature_width), bf16),
+            pltpu.VMEM((members, groups, keep, width), bf16),
+            pltpu.VMEM((2 * tok_rows, feature_width), jnp.float32),
+            pltpu.VMEM((2 * tok_rows, feature_width), bf16),
+            pltpu.VMEM((chips, 2 * tok_rows, w_qkv.shape[1]), bf16),
             pltpu.VMEM((members, row_total, width), bf16),
             pltpu.VMEM((chips, row_total, width), bf16),
             pltpu.VMEM((chips, row_total, width), bf16),
             pltpu.VMEM((chips - 1, row_total, width), bf16),
             pltpu.VMEM((groups, keep, width), bf16),
-            pltpu.VMEM((groups, keep, width), bf16),
-            dma((4,)),
+            dma((5,)),
             dma,
             dma,
             dma((3,)),
             dma((3,)),
             dma((groups - 1,)),
             dma((groups - 1,)),
+            dma((12,)),
+            dma((12,)),
             dma((10,)),
             dma((10,)),
-            dma((10,)),
-            dma((10,)),
-            dma((2,)),
+            dma((chips,)),
         ],
         compiler_params=pltpu.CompilerParams(
             collective_id=0, has_side_effects=True, vmem_limit_bytes=60 * 1024 * 1024
         ),
-    )(inputs, gates[:, :, None], table, gate_t, up_t, w_down, residual)
+    )(inputs, gates[:, :, None], table, gate_t, up_t, w_down, residual, slots, gain, w_qkv)
 
 
 def plain_rows(
@@ -452,7 +509,7 @@
     same = jnp.eye(local_experts, dtype=jnp.bfloat16)
     send_table = send_table[:, :, :, None, :] * same[None, :, None, :, None]
     if tensor_count == 8:
-        residual_all, rows = communicate(
+        return communicate(
             expert_count,
             tensor_count,
             send_table.reshape(expert_count, local_experts * keep, -1),
@@ -462,18 +519,15 @@
             w_up,
             w_down,
             residual,
-        )
-        residual_all = residual_all.reshape(group_rows, feature_width)
-        rows = rows.reshape(tensor_count, -1, feature_width // tensor_count)
-        chips = tensor_count // 2
-        order = tuple((c % chips) * 2 + c // chips for c in range(tensor_count))
-    else:
-        residual_all = lax.all_gather(residual, "tensor", axis=0, tiled=True)
-        rows = plain_rows(
-            expert_inputs, gates, w_gate, w_up, w_down, send_table, expert_count, tensor_count
-        )
-        order = tuple(range(tensor_count))
-
+            token_at,
+            norm_gain[None, :],
+            w_qkv,
+        )
+    residual_all = lax.all_gather(residual, "tensor", axis=0, tiled=True)
+    rows = plain_rows(
+        expert_inputs, gates, w_gate, w_up, w_down, send_table, expert_count, tensor_count
+    )
+    order = tuple(range(tensor_count))
     return finish(
         lax.axis_index("tensor").reshape(1),
         token_at,

time: 90.3 us -> 87.3 us (0.967)
  Pallas kernels: 84.2 us -> 75.2 us
  local copies, waits for them, and re-layouts: 2.45 us -> 8.48 us
    pallas_call x2 -> x1, Pallas kernels: 84.2 us -> 75.2 us  [communicate(): pl.pallas_call(functools.partial(comm_kernel, groups), in_specs=[vmem] *...]
    unnamed x0 -> x2, local copies, waits for them, and re-layouts: none -> 6.04 us
where the time goes in v3:
time: 87.3 us; the launch traced here: 87 us
  Pallas kernels  75.2 us (86%)
  local copies, waits for them, and re-layouts  8.48 us (10%)
  other arithmetic  2.62 us (3%)
    pallas_call x1, Pallas kernels, communicate(): pl.pallas_call(functools.partial(comm_kernel, groups), in_specs=[vmem] *...  75.2 us
    unnamed x2, local copies, waits for them, and re-layouts  6.04 us

profile of v3, /device:TPU:0, one launch (start us, length us, event | category | flops | bytes accessed | tf_op | source)
XLA Modules:
  0.0 87.0 jit_solution(8602510105962986900)
XLA Ops:
  0.6 0.7 add_select_fusion.1
  1.4 0.3 convert_reduce_fusion
  1.7 0.7 compare_select_fusion
  2.4 0.2 select_reduce_fusion
  2.6 0.6 sub.14.slots_ref
  3.3 0.1 mul.27
  3.4 0.1 mul.28
  3.5 0.1 mul.25
  3.6 0.1 mul.26
  3.7 0.6 broadcast_multiply_fusion.table_ref
  4.4 1.4 %copy.12.gates_ref = f32[2,64,1]{2,1,0:T(8,128)} copy(f32[2,64,1]{1,0,2:T(2,128)} %bitcast.7) | data formatting | bytes 1024 | tf_op jit(solution)/shard_map/broadcast_in_dim | solution.py:438
  5.8 75.2 %shard_map.104 = (bf16[128,4096]{1,0:T(8,128)(2,1)}, bf16[1024,1536]{1,0:T(8,128)(2,1)}) custom-call(bf16[2,64,4096]{2,1,0:T(8,128)(2,1)} %inputs_ref.1, f32[2,64,1]{2,1,0:T(8,128)} %copy.12.gates_ref, bf16[4,64,128]{2,1,0:T(8,128)(2,1)} %broadcast_multiply_fusion.table_ref, bf16[2,224,4096]{2,1,0:T(8,128)(2,1)} %bitcast.4, bf16[2,224,4096]{2,1,0:T(8,128)(2,1)} %bitcast.5, ...), custom_call_target="tpu_custom_call" | custom-call | tf_op jit(solution)/shard_map/pallas_call | solution.py:399
  81.0 2.3 %copy.15 = bf16[128,4096]{1,0:T(8,128)(2,1)} copy(bf16[128,4096]{1,0:T(8,128)(2,1)} %get-tuple-element.8) | data formatting | bytes 2097152
  83.3 3.8 %copy.16 = bf16[1024,1536]{1,0:T(8,128)(2,1)} copy(bf16[1024,1536]{1,0:T(8,128)(2,1)} %get-tuple-element.9) | data formatting | bytes 6291456
  (7 shorter events, 0.1 us)

commit v4 on v3

--- a/solution.py
+++ b/solution.py
@@ -304,15 +304,16 @@
 
     pair = 2 * tok_rows
     slot_total = slots_ref.shape[1]
-    tile = 256
+    tile = 512
     col_tiles = weight.shape[1] // tile
     stores = []
 
     def finish_pair(step, chip):
+        tokens = lax.broadcasted_iota(jnp.int32, (pair, slot_total), 0) + chip * pair
+        placement = jnp.where(slots_ref[...] == tokens, 1.0, 0.0).astype(jnp.bfloat16)
+
         def place(index, squares):
             cols = pl.ds(pl.multiple_of(index * width, width), width)
-            tokens = lax.broadcasted_iota(jnp.int32, (pair, slot_total), 0) + chip * pair
-            placement = jnp.where(slots_ref[...] == tokens, 1.0, 0.0).astype(jnp.bfloat16)
             source = (index % chips) * 2 + index // chips
             values = rows[source].reshape(slot_total, width)
             block = blocks[pl.ds(2 * chip, 2), :, cols].reshape(pair, width)
@@ -325,7 +326,7 @@
                 squares = squares + piece * piece
             return squares
 
-        squares = lax.fori_loop(0, 2 * chips, place, jnp.zeros((pair, 128), jnp.float32))
+        squares = lax.fori_loop(0, 2 * chips, place, jnp.zeros((pair, 128), jnp.float32), unroll=2)
         scale = lax.rsqrt(jnp.sum(squares, axis=1, keepdims=True) / feature_width + 1e-06)
 
         def norm(index, carry):
@@ -335,7 +336,7 @@
             )
             return carry
 
-        lax.fori_loop(0, 2 * chips, norm, 0)
+        lax.fori_loop(0, 2 * chips, norm, 0, unroll=2)
         if step == 0:
             begin = pl.multiple_of(core * tok_rows, tok_rows)
             stream_ref[...] = combined_ref[pl.ds(begin, tok_rows), :].astype(jnp.bfloat16)

time: 87.3 us -> 82.1 us (0.940)
  Pallas kernels: 75.2 us -> 70 us
    pallas_call x1, Pallas kernels: 75.2 us -> 70 us  [communicate(): pl.pallas_call(functools.partial(comm_kernel, groups), in_specs=[vmem] *...]
where the time goes in v4:
time: 82.1 us; the launch traced here: 81.8 us
  Pallas kernels  70 us (85%)
  local copies, waits for them, and re-layouts  8.48 us (10%)
  other arithmetic  2.62 us (3%)
    pallas_call x1, Pallas kernels, communicate(): pl.pallas_call(functools.partial(comm_kernel, groups), in_specs=[vmem] *...  70 us
    unnamed x2, local copies, waits for them, and re-layouts  6.04 us

profile of v4, /device:TPU:0, one launch (start us, length us, event | category | flops | bytes accessed | tf_op | source)
XLA Modules:
  0.0 81.8 jit_solution(1705309520412523330)
XLA Ops:
  0.6 0.7 add_select_fusion.1
  1.4 0.3 convert_reduce_fusion
  1.7 0.7 compare_select_fusion
  2.4 0.2 select_reduce_fusion
  2.6 0.6 sub.14.slots_ref
  3.3 0.1 mul.27
  3.4 0.1 mul.28
  3.5 0.1 mul.25
  3.6 0.1 mul.26
  3.7 0.6 broadcast_multiply_fusion.table_ref
  4.4 1.4 %copy.12.gates_ref = f32[2,64,1]{2,1,0:T(8,128)} copy(f32[2,64,1]{1,0,2:T(2,128)} %bitcast.7) | data formatting | bytes 1024 | tf_op jit(solution)/shard_map/broadcast_in_dim | solution.py:439
  5.8 70.0 %shard_map.104 = (bf16[128,4096]{1,0:T(8,128)(2,1)}, bf16[1024,1536]{1,0:T(8,128)(2,1)}) custom-call(bf16[2,64,4096]{2,1,0:T(8,128)(2,1)} %inputs_ref.1, f32[2,64,1]{2,1,0:T(8,128)} %copy.12.gates_ref, bf16[4,64,128]{2,1,0:T(8,128)(2,1)} %broadcast_multiply_fusion.table_ref, bf16[2,224,4096]{2,1,0:T(8,128)(2,1)} %bitcast.4, bf16[2,224,4096]{2,1,0:T(8,128)(2,1)} %bitcast.5, ...), custom_call_target="tpu_custom_call" | custom-call | tf_op jit(solution)/shard_map/pallas_call | solution.py:400
  75.8 2.3 %copy.15 = bf16[128,4096]{1,0:T(8,128)(2,1)} copy(bf16[128,4096]{1,0:T(8,128)(2,1)} %get-tuple-element.8) | data formatting | bytes 2097152
  78.1 3.8 %copy.16 = bf16[1024,1536]{1,0:T(8,128)(2,1)} copy(bf16[1024,1536]{1,0:T(8,128)(2,1)} %get-tuple-element.9) | data formatting | bytes 6291456
  (7 shorter events, 0.1 us)
